TPU v7x, 32 devices: a whole 2x2x4 slice. The times are simulated.
32 devices in a mesh: groups: 2 (over y), blk: 16 (over z, x, core).
Axes of the slice: x: 2, y: 2, z: 4, core: 2. Of those that a mesh axis runs over, the one named last changes fastest.
Arguments:
- queries: bfloat16 [8192, 2560], P(('groups', 'blk')), parts along dimension 0
- keys: bfloat16 [8192, 2560], P(('groups', 'blk')), parts along dimension 0
- values: bfloat16 [8192, 2560], P(('groups', 'blk')), parts along dimension 0
- out_weight: bfloat16 [64, 2560], replicated, may hold values from -0.125 to 0.125
- latent: float32 [64, 8192], P(None, ('groups', 'blk')), parts along dimension 1, may hold values from -6 to 6
- valid: int32 [32], P('groups'), parts along dimension 0, may hold values from 64 to 256, as said below
- timestep: int32 [2], P('groups'), parts along dimension 0, may hold values from 0 to 9
Outputs:
- velocity: float32 [64, 8192], P(None, ('groups', 'blk')), parts along dimension 1
- latent_next: float32 [64, 8192], P(None, ('groups', 'blk')), parts along dimension 1
There are 2 independent parts, one for each index of `groups`. A program takes and returns all parts, laid end to end along the dimension named above; an argument that names none is the same for every part. Nothing has to cross between parts.
Inputs may be any that keep to these rules, and one draw needn't show every extreme that they name: `valid`: blocks whose index is one less than a multiple of 4 hold between 64 and 256 used tokens; all other blocks are full.
All inputs are finite; a program needn't handle non-finite values.
Results may differ from a plain program's by a relative error of at most 0.0065.
Values may be sent and summed in bfloat16 or wider, within the bound.
A program may use at most 128 MiB of HBM per device.

v0:
```python
import jax
import jax.numpy as jnp
from jax import lax
from jax.sharding import PartitionSpec as P

HEADS = 20
HEAD_DIM = 128
LATENT_CH = 64
R_WIN = 2
STEPS = 10


def shifted(shard, axis, by):
    length = lax.axis_size(axis)
    pairs = [(i, i + by) for i in range(length) if 0 <= i + by < length]
    return lax.ppermute(shard, axis, pairs)


def local(queries, keys, values, out_weight, latent, valid, timestep):
    row_count = queries.shape[0]
    own_index = lax.axis_index("blk")
    block_total = lax.axis_size("blk")
    score_scale = 1.0 / jnp.sqrt(jnp.float32(HEAD_DIM))
    query_heads = queries.reshape(row_count, HEADS, HEAD_DIM)
    slots = jnp.arange(row_count, dtype=jnp.int32)

    def block_scores(key_value, block):
        inside = (block >= 0) & (block < block_total)
        filled = jnp.where(inside, valid[jnp.clip(block, 0, block_total - 1)], 0)
        key_heads = key_value[0].reshape(row_count, HEADS, HEAD_DIM)
        scores = (
            jnp.einsum("qhd,khd->hqk", query_heads, key_heads, preferred_element_type=jnp.float32)
            * score_scale
        )
        return jnp.where((slots < filled)[None, None, :], scores, jnp.float32(-1e30))

    def weighted(weights, key_value):
        value_heads = key_value[1].reshape(row_count, HEADS, HEAD_DIM)
        return jnp.einsum(
            "hqk,khd->hqd",
            weights.astype(jnp.bfloat16),
            value_heads,
            preferred_element_type=jnp.float32,
        )

    def absorb(carry, key_value, block):
        run_max, run_sum, run_out = carry
        scores = block_scores(key_value, block)
        new_max = jnp.maximum(run_max, jnp.max(scores, axis=-1))
        shrink = jnp.exp(run_max - new_max)
        weights = jnp.exp(scores - new_max[:, :, None])
        run_sum = run_sum * shrink + jnp.sum(weights, axis=-1)
        run_out = run_out * shrink[:, :, None] + weighted(weights, key_value)
        return (new_max, run_sum, run_out)

    own_pair = (keys, values)
    own_scores = block_scores(own_pair, own_index)
    own_max = jnp.max(own_scores, axis=-1)
    own_weights = jnp.exp(own_scores - own_max[:, :, None])
    carry = (own_max, jnp.sum(own_weights, axis=-1), weighted(own_weights, own_pair))
    earlier = own_pair
    following = own_pair
    for distance in range(1, R_WIN + 1):
        earlier = shifted((earlier[0], earlier[1]), "blk", 1)
        following = shifted((following[0], following[1]), "blk", -1)
        carry = absorb(carry, earlier, own_index - distance)
        carry = absorb(carry, following, own_index + distance)
    run_max, run_sum, run_out = carry
    mixed = run_out / run_sum[:, :, None]
    mixed = jnp.transpose(mixed, (1, 0, 2)).reshape(row_count, HEADS * HEAD_DIM)
    used = slots < valid[own_index]
    attn = jnp.where(used[:, None], mixed, 0.0).astype(jnp.bfloat16)
    vel = lax.dot_general(
        out_weight, attn, (((1,), (1,)), ((), ())), preferred_element_type=jnp.float32
    )
    squares = lax.psum(jnp.sum(vel * vel), "blk")
    count = jnp.float32(LATENT_CH) * jnp.sum(valid.astype(jnp.float32))
    rms = jnp.sqrt(squares / count + 1e-06)
    velocity = vel / rms
    level = timestep[0].astype(jnp.float32)
    early = 1.0 - level / STEPS
    later = 1.0 - (level + 1.0) / STEPS
    sigma_early = 5.0 * early / (1.0 + 4.0 * early)
    sigma_later = 5.0 * later / (1.0 + 4.0 * later)
    return (velocity, latent + (sigma_later - sigma_early) * velocity)


def solution(mesh):
    in_specs = (
        P(("groups", "blk"), None),
        P(("groups", "blk"), None),
        P(("groups", "blk"), None),
        P(),
        P(None, ("groups", "blk")),
        P("groups"),
        P("groups"),
    )
    out_specs = (P(None, ("groups", "blk")), P(None, ("groups", "blk")))
    return jax.shard_map(local, mesh=mesh, in_specs=in_specs, out_specs=out_specs, check_vma=False)
```

profile of v0, /device:TPU:0, one launch (start us, length us, event | category | flops | bytes accessed | tf_op | source)
XLA Modules:
  0.0 174.4 jit_solution(11538853951131140014)
XLA Ops:
  0.6 0.0 copy-start
  0.6 0.0 copy-start.8
  0.7 1.6 copy.26
  2.3 1.3 collective-permute-start.2
  3.6 4.1 %collective-permute-start = (bf16[256,2560]{0,1:T(8,128)(2,1)S(1)}, bf16[256,2560]{0,1:T(8,128)(2,1)}, u32[]{:S(2)}, u32[]{:S(2)}) collective-permute-start(bf16[256,2560]{0,1:T(8,128)(2,1)S(1)} %copy.26), channel_id=1, source_target_pairs={{0,1},{1,2},{2,3},{3,4},{4,5},{5,6},{6,7},{7,8},{8,9},{9,10},{10,1... | collective-permute-start | bytes 3932168 | tf_op jit(solution)/shard_map/ppermute | solution.py:16
  7.8 4.5 %collective-permute-start.1 = (bf16[256,2560]{1,0:T(8,128)(2,1)}, bf16[256,2560]{1,0:T(8,128)(2,1)}, u32[]{:S(2)}, u32[]{:S(2)}) collective-permute-start(bf16[256,2560]{1,0:T(8,128)(2,1)} %param.9), channel_id=1, source_target_pairs={{0,1},{1,2},{2,3},{3,4},{4,5},{5,6},{6,7},{7,8},{8,9},{9,10},{10,1... | collective-permute-start | bytes 3932168 | tf_op jit(solution)/shard_map/ppermute | solution.py:16
  12.2 1.3 collective-permute-start.3
  13.5 2.4 %copy.29 = bf16[256,2560]{0,1:T(8,128)(2,1)} copy(bf16[256,2560]{1,0:T(8,128)(2,1)} %param.9) | data formatting | bytes 2621440 | tf_op args[2]
  16.0 0.0 copy-done.8
  16.0 0.7 fusion.70
  17.3 1.6 copy.25
  21.5 0.6 convert_reduce_fusion
  22.1 0.0 copy-start.4
  22.1 1.4 fusion
  23.4 0.0 copy-done.4
  23.5 2.9 %fusion.23 = f32[20,256,128]{1,2,0:T(8,128)} fusion(bf16[256,20,128]{0,2,1:T(8,128)(2,1)S(1)} %bitcast.161, f32[20,256,256]{1,2,0:T(8,128)S(1)} %get-tuple-element.26, f32[20,256]{1,0:T(8,128)S(1)} %get-tuple-element.25, pred[256]{0:T(512)(128)(4,1)S(1)} %iota_compare_fusion.4), kind=kOutput, calls=%fused_computation.29 | convolution fusion | flops 340787200 | bytes 9195776 | tf_op jit(solution)/shard_map/hqk,khd->hqd/dot_general | solution.py:39
  26.3 0.0 collective-permute-done.2
  26.3 1.3 collective-permute-start.6
  27.6 1.2 fusion.5
  28.8 0.0 collective-permute-done
  28.8 39.0 %collective-permute-start.4 = (bf16[256,2560]{0,1:T(8,128)(2,1)}, bf16[256,2560]{0,1:T(8,128)(2,1)}, u32[]{:S(2)}, u32[]{:S(2)}) collective-permute-start(bf16[256,2560]{0,1:T(8,128)(2,1)} %collective-permute-done), channel_id=1, source_target_pairs={{0,1},{1,2},{2,3},{3,4},{4,5},{5,6},{6,7},{7,8},{8,9},{9,10},{10,1... | collective-permute-start | bytes 3932168 | tf_op jit(solution)/shard_map/ppermute | solution.py:16
  67.8 0.6 iota_compare_fusion.5
  69.9 0.0 collective-permute-done.1
  69.9 2.4 %copy.34 = bf16[256,2560]{0,1:T(8,128)(2,1)} copy(bf16[256,2560]{1,0:T(8,128)(2,1)} %collective-permute-done.1) | data formatting | bytes 2621440 | tf_op jit(solution)/shard_map/ppermute | solution.py:16
  72.3 12.1 %collective-permute-start.5 = (bf16[256,2560]{1,0:T(8,128)(2,1)}, bf16[256,2560]{1,0:T(8,128)(2,1)}, u32[]{:S(2)}, u32[]{:S(2)}) collective-permute-start(bf16[256,2560]{1,0:T(8,128)(2,1)} %collective-permute-done.1), channel_id=1, source_target_pairs={{0,1},{1,2},{2,3},{3,4},{4,5},{5,6},{6,7},{7,8},{8,9},{9,10},{10,1... | collective-permute-start | bytes 3932168 | tf_op jit(solution)/shard_map/ppermute | solution.py:16
  84.4 0.0 collective-permute-done.3
  84.4 1.6 copy.39
  86.0 1.3 collective-permute-start.7
  87.3 2.7 %fusion.2 = (f32[20,256]{1,0:T(8,128)S(1)}, f32[20,256,256]{1,2,0:T(8,128)S(1)}) fusion(pred[256]{0:T(512)(128)(4,1)S(1)} %iota_compare_fusion.2, bf16[256,20,128]{0,2,1:T(8,128)(2,1)S(1)} %bitcast.154, bf16[256,20,128]{0,2,1:T(8,128)(2,1)} %bitcast.13), kind=kOutput, calls=%fused_computation.12 | convolution fusion | flops 339471360 | bytes 7885056 | tf_op jit(solution)/shard_map/qhd,khd->hqk/dot_general | solution.py:32
  90.0 0.0 copy-start.1
  90.0 3.7 %fusion.1 = (f32[20,256]{1,0:T(8,128)S(1)}, f32[20,256,256]{1,2,0:T(8,128)S(1)}) fusion(pred[256]{0:T(512)(128)(4,1)S(1)} %iota_compare_fusion.3, bf16[256,20,128]{0,2,1:T(8,128)(2,1)S(1)} %bitcast.155, bf16[256,20,128]{0,2,1:T(8,128)(2,1)} %bitcast.8), kind=kOutput, calls=%fused_computation.11 | convolution fusion | flops 339471360 | bytes 7885056 | tf_op jit(solution)/shard_map/qhd,khd->hqk/dot_general | solution.py:32
  93.7 0.0 collective-permute-done.6
  93.7 2.7 %fusion.4 = (f32[20,256]{1,0:T(8,128)S(1)}, f32[20,256,256]{1,2,0:T(8,128)S(1)}) fusion(pred[256]{0:T(512)(128)(4,1)S(1)} %iota_compare_fusion, bf16[256,20,128]{0,2,1:T(8,128)(2,1)S(1)} %bitcast.156, bf16[256,20,128]{0,2,1:T(8,128)(2,1)} %bitcast.23), kind=kOutput, calls=%fused_computation.14 | convolution fusion | flops 339471360 | bytes 7885056 | tf_op jit(solution)/shard_map/qhd,khd->hqk/dot_general | solution.py:32
  96.4 0.0 copy-start.3
  96.4 0.0 collective-permute-done.4
  96.4 3.7 %fusion.3 = (f32[20,256]{1,0:T(8,128)S(1)}, f32[20,256,256]{1,2,0:T(8,128)S(1)}) fusion(pred[256]{0:T(512)(128)(4,1)S(1)} %iota_compare_fusion.1, bf16[256,20,128]{0,2,1:T(8,128)(2,1)S(1)} %bitcast.157, bf16[256,20,128]{0,2,1:T(8,128)(2,1)} %bitcast.18), kind=kOutput, calls=%fused_computation.13 | convolution fusion | flops 339471360 | bytes 7885056 | tf_op jit(solution)/shard_map/qhd,khd->hqk/dot_general | solution.py:32
  100.1 0.0 copy-start.2
  100.1 0.0 copy-done.1
  100.1 2.8 %fusion.7 = (f32[20,256]{1,0:T(8,128)S(1)}, f32[20,256]{1,0:T(8,128)S(1)}) fusion(f32[20,256,256]{1,2,0:T(8,128)S(1)} %get-tuple-element.28, f32[20,256]{1,0:T(8,128)S(1)} %get-tuple-element.12, pred[256]{0:T(512)(128)(4,1)S(1)} %iota_compare_fusion.3, f32[20,256]{1,0:T(8,128)S(1)} %get-tuple-element.11, f32[20,256,256]{1,2,0:T(8,128)S(1)} %get-tuple-element.24, ...), kind=kLoop, calls=%fused_computation.17 | loop fusion | flops 10475520 | bytes 10568192 | tf_op jit(solution)/shard_map/reduce_sum | solution.py:52
  102.9 0.0 copy-done.3
  103.0 0.0 copy-done.2
  103.0 0.0 copy-start.5
  103.0 2.7 %fusion.11 = (f32[20,256]{1,0:T(8,128)S(1)}, f32[20,256]{1,0:T(8,128)S(1)}) fusion(f32[20,256,256]{1,2,0:T(8,128)S(1)} %get-tuple-element.22, f32[20,256]{1,0:T(8,128)S(1)} %get-tuple-element.10, pred[256]{0:T(512)(128)(4,1)S(1)} %iota_compare_fusion.1, f32[20,256]{1,0:T(8,128)S(1)} %get-tuple-element.9, f32[20,256,256]{1,2,0:T(8,128)S(1)} %get-tuple-element.20, ...), kind=kLoop, calls=%fused_computation.21 | loop fusion | flops 10475520 | bytes 10568192 | tf_op jit(solution)/shard_map/reduce_sum | solution.py:52
  105.7 0.0 copy-done.5
  105.7 2.8 %fusion.21 = f32[20,256,128]{1,2,0:T(8,128)} fusion(bf16[256,20,128]{0,2,1:T(8,128)(2,1)S(1)} %bitcast.163, f32[20,256,256]{1,2,0:T(8,128)S(1)} %get-tuple-element.28, f32[20,256]{1,0:T(8,128)S(1)} %get-tuple-element.12, pred[256]{0:T(512)(128)(4,1)S(1)} %iota_compare_fusion.3), kind=kOutput, calls=%fused_computation.28 | convolution fusion | flops 340787200 | bytes 9195776 | tf_op jit(solution)/shard_map/hqk,khd->hqd/dot_general | solution.py:39
  108.5 0.0 collective-permute-done.5
  108.5 1.6 copy.43
  110.1 0.0 slice-start
  110.2 0.0 slice-start.1
  110.2 5.5 %fusion.19 = f32[20,256,128]{1,2,0:T(8,128)} fusion(bf16[256,20,128]{0,2,1:T(8,128)(2,1)S(1)} %bitcast.162, f32[20,256,256]{1,2,0:T(8,128)} %copy-done.1, f32[20,256]{1,0:T(8,128)S(1)} %get-tuple-element.11, pred[256]{0:T(512)(128)(4,1)S(1)} %iota_compare_fusion.2), kind=kOutput, calls=%fused_computation.27 | convolution fusion | flops 340787200 | bytes 9195776 | tf_op jit(solution)/shard_map/hqk,khd->hqd/dot_general | solution.py:39
  115.7 0.0 slice-done
  115.7 0.0 slice-done.1
  115.7 2.9 %fusion.17 = f32[20,256,128]{1,2,0:T(8,128)} fusion(bf16[256,20,128]{0,2,1:T(8,128)(2,1)S(1)} %bitcast.164, f32[20,256,256]{1,2,0:T(8,128)S(1)} %bitcast.159, f32[20,256]{1,0:T(8,128)S(1)} %get-tuple-element.10, pred[256]{0:T(512)(128)(4,1)S(1)} %iota_compare_fusion.1), kind=kOutput, calls=%fused_computation.26 | convolution fusion | flops 340787200 | bytes 9195776 | tf_op jit(solution)/shard_map/hqk,khd->hqd/dot_general | solution.py:39
  118.6 0.0 collective-permute-done.7
  118.6 2.6 %copy.47 = bf16[256,2560]{0,1:T(8,128)(2,1)} copy(bf16[256,2560]{1,0:T(8,128)(2,1)} %collective-permute-done.7) | data formatting | bytes 2621440 | tf_op jit(solution)/shard_map/ppermute | solution.py:16
  121.2 0.0 copy-done.6
  121.2 7.2 %fusion.26 = bf16[256,20,128]{0,2,1:T(8,128)(2,1)S(1)} fusion(f32[20,256,128]{1,2,0:T(8,128)} %fusion.17, f32[20,256,128]{1,2,0:T(8,128)} %fusion.19, f32[20,256,128]{1,2,0:T(8,128)} %fusion.21, f32[20,256,128]{1,2,0:T(8,128)S(1)} %copy-done.6, f32[256,20]{0,1:T(8,128)S(1)} %get-tuple-element.4, f32[256,20]{0,1:T(8,128)S(1)} %get-tuple-element.8, ...), kind=kOutput, calls=%fused_computation.33 | convolution fusion | flops 347340800 | bytes 18473216 | tf_op jit(solution)/shard_map/hqk,khd->hqd/dot_general | solution.py:39
  128.4 0.0 copy-start.7
  128.5 0.3 fusion.25
  128.8 0.0 copy-done
  128.8 1.0 multiply_reduce_fusion
  129.7 43.2 %psum.7 = f32[]{:T(128)} all-reduce(f32[]{:T(128)} %get-tuple-element.29), channel_id=1, replica_groups=mesh['groups'=2,'blk'=16] {'blk'}, use_global_device_ids=true, to_apply=%region_11.12 | all-reduce | flops 1 | bytes 8 | tf_op jit(solution)/shard_map/psum | solution.py:76
  173.7 0.0 copy-done.7
  173.7 0.7 multiply_add_fusion
  (9 shorter events, 0.1 us)
Async XLA Ops:
  0.6 128.2 %copy-start = (bf16[64,2560]{1,0:T(8,128)(2,1)S(1)}, bf16[64,2560]{1,0:T(8,128)(2,1)}, u32[]{:S(2)}) copy-start(bf16[64,2560]{1,0:T(8,128)(2,1)} %param.10) | copy-start | bytes 983044
  0.6 15.3 %copy-start.8 = (s32[16]{0:T(128)S(1)}, s32[16]{0:T(128)}, u32[]{:S(2)}) copy-start(s32[16]{0:T(128)} %param.12) | copy-start | bytes 196
  2.3 24.0 %collective-permute-start.2 = (bf16[256,2560]{0,1:T(8,128)(2,1)S(1)}, bf16[256,2560]{0,1:T(8,128)(2,1)}, u32[]{:S(2)}, u32[]{:S(2)}) collective-permute-start(bf16[256,2560]{0,1:T(8,128)(2,1)S(1)} %copy.26), channel_id=1, source_target_pairs={{1,0},{2,1},{3,2},{4,3},{5,4},{6,5},{7,6},{8,7},{9,8},{10,9},{11,1... | collective-permute-start | bytes 3932168 | tf_op jit(solution)/shard_map/ppermute | solution.py:16
  3.6 25.2 %collective-permute-start = (bf16[256,2560]{0,1:T(8,128)(2,1)S(1)}, bf16[256,2560]{0,1:T(8,128)(2,1)}, u32[]{:S(2)}, u32[]{:S(2)}) collective-permute-start(bf16[256,2560]{0,1:T(8,128)(2,1)S(1)} %copy.26), channel_id=1, source_target_pairs={{0,1},{1,2},{2,3},{3,4},{4,5},{5,6},{6,7},{7,8},{8,9},{9,10},{10,1... | collective-permute-start | bytes 3932168 | tf_op jit(solution)/shard_map/ppermute | solution.py:16
  7.8 62.1 %collective-permute-start.1 = (bf16[256,2560]{1,0:T(8,128)(2,1)}, bf16[256,2560]{1,0:T(8,128)(2,1)}, u32[]{:S(2)}, u32[]{:S(2)}) collective-permute-start(bf16[256,2560]{1,0:T(8,128)(2,1)} %param.9), channel_id=1, source_target_pairs={{0,1},{1,2},{2,3},{3,4},{4,5},{5,6},{6,7},{7,8},{8,9},{9,10},{10,1... | collective-permute-start | bytes 3932168 | tf_op jit(solution)/shard_map/ppermute | solution.py:16
  12.2 72.2 %collective-permute-start.3 = (bf16[256,2560]{1,0:T(8,128)(2,1)}, bf16[256,2560]{1,0:T(8,128)(2,1)}, u32[]{:S(2)}, u32[]{:S(2)}) collective-permute-start(bf16[256,2560]{1,0:T(8,128)(2,1)} %param.9), channel_id=1, source_target_pairs={{1,0},{2,1},{3,2},{4,3},{5,4},{6,5},{7,6},{8,7},{9,8},{10,9},{11,1... | collective-permute-start | bytes 3932168 | tf_op jit(solution)/shard_map/ppermute | solution.py:16
  22.1 1.4 copy-start.4
  26.3 67.3 %collective-permute-start.6 = (bf16[256,2560]{0,1:T(8,128)(2,1)}, bf16[256,2560]{0,1:T(8,128)(2,1)}, u32[]{:S(2)}, u32[]{:S(2)}) collective-permute-start(bf16[256,2560]{0,1:T(8,128)(2,1)} %collective-permute-done.2), channel_id=1, source_target_pairs={{1,0},{2,1},{3,2},{4,3},{5,4},{6,5},{7,6},{8,7},{9,8},{10,9},{11,1... | collective-permute-start | bytes 3932168 | tf_op jit(solution)/shard_map/ppermute | solution.py:16
  28.8 67.5 %collective-permute-start.4 = (bf16[256,2560]{0,1:T(8,128)(2,1)}, bf16[256,2560]{0,1:T(8,128)(2,1)}, u32[]{:S(2)}, u32[]{:S(2)}) collective-permute-start(bf16[256,2560]{0,1:T(8,128)(2,1)} %collective-permute-done), channel_id=1, source_target_pairs={{0,1},{1,2},{2,3},{3,4},{4,5},{5,6},{6,7},{7,8},{8,9},{9,10},{10,1... | collective-permute-start | bytes 3932168 | tf_op jit(solution)/shard_map/ppermute | solution.py:16
  72.3 36.2 %collective-permute-start.5 = (bf16[256,2560]{1,0:T(8,128)(2,1)}, bf16[256,2560]{1,0:T(8,128)(2,1)}, u32[]{:S(2)}, u32[]{:S(2)}) collective-permute-start(bf16[256,2560]{1,0:T(8,128)(2,1)} %collective-permute-done.1), channel_id=1, source_target_pairs={{0,1},{1,2},{2,3},{3,4},{4,5},{5,6},{6,7},{7,8},{8,9},{9,10},{10,1... | collective-permute-start | bytes 3932168 | tf_op jit(solution)/shard_map/ppermute | solution.py:16
  86.0 32.6 %collective-permute-start.7 = (bf16[256,2560]{1,0:T(8,128)(2,1)}, bf16[256,2560]{1,0:T(8,128)(2,1)}, u32[]{:S(2)}, u32[]{:S(2)}) collective-permute-start(bf16[256,2560]{1,0:T(8,128)(2,1)} %collective-permute-done.3), channel_id=1, source_target_pairs={{1,0},{2,1},{3,2},{4,3},{5,4},{6,5},{7,6},{8,7},{9,8},{10,9},{11,1... | collective-permute-start | bytes 3932168 | tf_op jit(solution)/shard_map/ppermute | solution.py:16
  90.0 10.1 %copy-start.1 = (f32[20,256,256]{1,2,0:T(8,128)}, f32[20,256,256]{1,2,0:T(8,128)S(1)}, u32[]{:S(2)}) copy-start(f32[20,256,256]{1,2,0:T(8,128)S(1)} %get-tuple-element.24) | copy-start | bytes 15728644
  96.4 6.6 %copy-start.3 = (f32[20,256,256]{1,2,0:T(8,128)}, f32[20,256,256]{1,2,0:T(8,128)S(1)}, u32[]{:S(2)}) copy-start(f32[20,256,256]{1,2,0:T(8,128)S(1)} %get-tuple-element.20) | copy-start | bytes 15728644
  100.1 2.9 %copy-start.2 = (f32[20,256,256]{1,2,0:T(8,128)}, f32[20,256,256]{1,2,0:T(8,128)S(1)}, u32[]{:S(2)}) copy-start(f32[20,256,256]{1,2,0:T(8,128)S(1)} %get-tuple-element.22) | copy-start | bytes 15728644
  103.0 2.7 %copy-start.5 = (bf16[256,2560]{0,1:T(8,128)(2,1)S(1)}, bf16[256,2560]{0,1:T(8,128)(2,1)}, u32[]{:S(2)}) copy-start(bf16[256,2560]{0,1:T(8,128)(2,1)} %copy.34) | copy-start | bytes 3932164
  110.1 5.6 %slice-start = ((s8[5242880]{0:T(1024)(128)(4,1)}), s8[4194304]{0:T(1024)(128)(4,1)S(1)}, s32[]{:S(2)}) async-start(s8[5242880]{0:T(1024)(128)(4,1)} %bitcast.158), calls=%async_computation | async-start | bytes 8388608
  110.2 5.6 %slice-start.1 = ((s8[5242880]{0:T(1024)(128)(4,1)}), s8[1048576]{0:T(1024)(128)(4,1)S(1)}, s32[]{:S(2)}) async-start(s8[5242880]{0:T(1024)(128)(4,1)} %bitcast.158), calls=%async_computation.1 | async-start | bytes 2097152
  118.6 2.6 %copy-start.6 = (f32[20,256,128]{1,2,0:T(8,128)S(1)}, f32[20,256,128]{1,2,0:T(8,128)}, u32[]{:S(2)}) copy-start(f32[20,256,128]{1,2,0:T(8,128)} %fusion.23) | copy-start | bytes 7864324
  128.4 45.3 %copy-start.7 = (f32[64,256]{1,0:T(8,128)S(1)}, f32[64,256]{1,0:T(8,128)}, u32[]{:S(2)}) copy-start(f32[64,256]{1,0:T(8,128)} %param.11) | copy-start | bytes 196612
where the time goes:
time: 175 us; the launch traced here: 174 us
  starting transfers between devices  64.8 us (37%)
  blocking collectives  43.2 us (25%)
  matrix products  36.4 us (21%)
  local copies, waits for them, and re-layouts  14.6 us (8%)
  other arithmetic  9.02 us (5%)
  between operations  6.28 us (4%)
    ppermute x8, starting transfers between devices, shifted(): return lax.ppermute(shard, axis, pairs)  64.8 us
    psum x1, blocking collectives, local(): squares = lax.psum(jnp.sum(vel * vel), 'blk')  43.2 us
    dot_general x5, matrix products, weighted(): jnp.einsum('hqk,khd->hqd', weights.astype(jnp.bfloat16), value_heads, pre...  21.4 us
    dot_general x5, matrix products, block_scores(): jnp.einsum('qhd,khd->hqk', query_heads, key_heads, preferred_element_type...  14 us
    ppermute x4, local copies, waits for them, and re-layouts, shifted(): return lax.ppermute(shard, axis, pairs)  8.15 us
    unnamed x25, local copies, waits for them, and re-layouts  5.73 us
    reduce_sum x2, other arithmetic, absorb(): run_sum = run_sum * shrink + jnp.sum(weights, axis=-1)  5.51 us
  transfers between devices with their start and end apart: 8, of which 0 were waited for; matrix products, arithmetic and copies ran while one was open for 27% of the time, Pallas kernels for 0%

commit v1 on v0

v1 whole, which is shorter than its diff:
```python
import functools

import jax
import jax.numpy as jnp
from jax import lax
from jax.experimental import pallas as pl
from jax.experimental.pallas import tpu as pltpu
from jax.sharding import PartitionSpec as P

HEAD_DIM = 128
R_WIN = 2
STEPS = 10
UNIT = 4
BF16, F32 = jnp.bfloat16, jnp.float32
NT = (((1,), (1,)), ((), ()))
LOG2E = 1.4426950408889634


def kernel(n, q_hbm, k_hbm, v_hbm, w_ref, valid_ref, vel_ref, sq_ref,
           v_buf, vw_own, qbuf, kbuf, vwbuf, s_buf, vel_acc, vel_in, sq_in,
           loc_sem, v_sem, xs_sem, xr_sem, zs_sem, zr_sem, vs_sem, vr_sem, ss_sem, sr_sem):
    rows = q_hbm.shape[0]
    heads = q_hbm.shape[1] // HEAD_DIM
    mine = heads // UNIT
    units = n // UNIT
    me = lax.axis_index("blk")
    unit = me // UNIT
    slot = me % UNIT
    chip, core = slot // 2, slot % 2
    partner = [slot, 2 * chip + 1 - core, 2 * (1 - chip) + core, 2 * (1 - chip) + 1 - core]

    barrier = pltpu.get_barrier_semaphore()

    @pl.loop(1, n)
    def _(d):
        pl.semaphore_signal(barrier, inc=1, device_id={"blk": (me + d) % n},
                            device_id_type=pl.DeviceIdType.MESH)

    v_copy = pltpu.make_async_copy(v_hbm, v_buf, v_sem)
    v_copy.start()

    def columns(t, j):
        return pl.ds(pl.multiple_of((t * mine + j) * HEAD_DIM, HEAD_DIM), HEAD_DIM)

    def local(j, kind):
        if kind == 0:
            return pltpu.make_async_copy(
                k_hbm.at[:, columns(slot, j)], kbuf.at[j, R_WIN + slot], loc_sem.at[0, j])
        if kind == 1:
            return pltpu.make_async_copy(
                vw_own.at[slot * mine + j], vwbuf.at[j, R_WIN + slot], loc_sem.at[1, j])
        return pltpu.make_async_copy(
            q_hbm.at[:, columns(slot, j)], qbuf.at[j, slot], loc_sem.at[2, j])

    def cross(d, j, kind):
        t = partner[d]
        if kind == 0:
            src, dst = k_hbm.at[:, columns(t, j)], kbuf.at[j, R_WIN + slot]
        elif kind == 1:
            src, dst = vw_own.at[t * mine + j], vwbuf.at[j, R_WIN + slot]
        else:
            src, dst = q_hbm.at[:, columns(t, j)], qbuf.at[j, slot]
        return pltpu.make_async_remote_copy(
            src_ref=src, dst_ref=dst, send_sem=xs_sem.at[d - 1, kind, j],
            recv_sem=xr_sem.at[d - 1, kind, j], device_id={"blk": unit * UNIT + t},
            device_id_type=pl.DeviceIdType.MESH)

    def along(up, j, kind):
        buf = kbuf if kind == 0 else vwbuf
        frm, to = (UNIT, 0) if up else (R_WIN, R_WIN + UNIT)
        return pltpu.make_async_remote_copy(
            src_ref=buf.at[j, pl.ds(frm, R_WIN)], dst_ref=buf.at[j, pl.ds(to, R_WIN)],
            send_sem=zs_sem.at[int(up), kind, j], recv_sem=zr_sem.at[int(up), kind, j],
            device_id={"blk": (me + (UNIT if up else n - UNIT)) % n},
            device_id_type=pl.DeviceIdType.MESH)

    @pl.loop(0, mine)
    def _(j):
        local(j, 0).start()
        local(j, 2).start()

    @pl.when(unit == 0)
    def _():
        kbuf[:, 0:R_WIN] = jnp.zeros((mine, R_WIN, rows, HEAD_DIM), BF16)
        vwbuf[:, 0:R_WIN] = jnp.zeros((mine, R_WIN) + vwbuf.shape[2:], BF16)

    @pl.when(unit == units - 1)
    def _():
        kbuf[:, R_WIN + UNIT:] = jnp.zeros((mine, R_WIN, rows, HEAD_DIM), BF16)
        vwbuf[:, R_WIN + UNIT:] = jnp.zeros((mine, R_WIN) + vwbuf.shape[2:], BF16)

    vel_acc[...] = jnp.zeros_like(vel_acc)
    v_copy.wait()
    for h in range(heads):
        cols = slice(h * HEAD_DIM, (h + 1) * HEAD_DIM)
        vw_own[h] = lax.dot_general(
            w_ref[:, cols], v_buf[:, cols], NT, preferred_element_type=F32).astype(BF16)

    pl.semaphore_wait(barrier, n - 1)

    @pl.loop(0, mine + 1)
    def _(j):
        @pl.when(j < mine)
        def _():
            for kind in (0, 1):
                for d in (2, 3, 1):
                    cross(d, j, kind).start()
            local(j, 1).start()

        @pl.when(j > 0)
        def _():
            for d in (2, 3, 1):
                cross(d, j - 1, 2).start()

    limits = []
    for kb in range(UNIT + 2 * R_WIN):
        block = unit * UNIT - R_WIN + kb
        filled = valid_ref[jnp.clip(block, 0, n - 1)]
        limits.append(jnp.where((block >= 0) & (block < n), filled, 0))
    factor = LOG2E / (HEAD_DIM ** 0.5)
    masked = (0, 1, R_WIN + UNIT - 1, R_WIN + UNIT, R_WIN + UNIT + 1)

    def attend(j):
        row_id = lax.broadcasted_iota(jnp.int32, (rows, rows), 0)
        for qs in range(UNIT):
            queries = qbuf[j, qs]
            top = None
            for kk in range(2 * R_WIN + 1):
                kb = qs + kk
                s = lax.dot_general(kbuf[j, kb], queries, NT, preferred_element_type=F32)
                if kb in masked:
                    s = jnp.where(row_id < limits[kb], s, F32(-1e30))
                s_buf[qs % 2, kk] = s
                part = jnp.max(s, axis=0, keepdims=True)
                top = part if top is None else jnp.maximum(top, part)
            total = None
            out = None
            for kk in range(2 * R_WIN + 1):
                e = jnp.exp2((s_buf[qs % 2, kk] - top) * factor)
                part = jnp.sum(e, axis=0, keepdims=True)
                total = part if total is None else total + part
                o = jnp.dot(vwbuf[j, qs + kk], e.astype(BF16), preferred_element_type=F32)
                out = o if out is None else out + o
            vel_acc[qs] += out / total

    @pl.loop(0, mine + 1)
    def _(j):
        @pl.when(j < mine)
        def _():
            for kind in (0, 1):
                local(j, kind).wait()
                for d in (1, 2, 3):
                    cross(d, j, kind).wait_recv()

            @pl.when(unit < units - 1)
            def _():
                along(True, j, 0).start()
                along(True, j, 1).start()

            @pl.when(unit > 0)
            def _():
                along(False, j, 0).start()
                along(False, j, 1).start()

        @pl.when(j > 0)
        def _():
            i = j - 1
            local(i, 2).wait()
            for d in (1, 2, 3):
                cross(d, i, 2).wait_recv()

            @pl.when(unit > 0)
            def _():
                along(True, i, 0).wait_recv()
                along(True, i, 1).wait_recv()

            @pl.when(unit < units - 1)
            def _():
                along(False, i, 0).wait_recv()
                along(False, i, 1).wait_recv()

            attend(i)

    def give(d):
        return pltpu.make_async_remote_copy(
            src_ref=vel_acc.at[partner[d]], dst_ref=vel_in.at[d - 1],
            send_sem=vs_sem.at[d - 1], recv_sem=vr_sem.at[d - 1],
            device_id={"blk": unit * UNIT + partner[d]},
            device_id_type=pl.DeviceIdType.MESH)

    for d in (2, 3, 1):
        give(d).start()
    vel = vel_acc[slot]
    for d in (1, 2, 3):
        give(d).wait_recv()
        vel = vel + vel_in[d - 1]
    col_id = lax.broadcasted_iota(jnp.int32, vel.shape, 1)
    vel = jnp.where(col_id < valid_ref[me], vel, F32(0))
    vel_ref[...] = vel
    sq_in[0] = jnp.sum((vel * vel).reshape(vel.shape[0] // 8, 8, vel.shape[1]), axis=0)

    def tell(d):
        return pltpu.make_async_remote_copy(
            src_ref=sq_in.at[0], dst_ref=sq_in.at[d],
            send_sem=ss_sem.at[d], recv_sem=sr_sem.at[d],
            device_id={"blk": (me + d) % n}, device_id_type=pl.DeviceIdType.MESH)

    @pl.loop(1, n)
    def _(d):
        tell(d).start()

    @pl.loop(0, mine)
    def _(j):
        for d in (1, 2, 3):
            for kind in (0, 1, 2):
                cross(d, j, kind).wait_send()

        @pl.when(unit < units - 1)
        def _():
            along(True, j, 0).wait_send()
            along(True, j, 1).wait_send()

        @pl.when(unit > 0)
        def _():
            along(False, j, 0).wait_send()
            along(False, j, 1).wait_send()

    for d in (1, 2, 3):
        give(d).wait_send()

    @pl.loop(1, n)
    def _(d):
        tell(d).wait()

    sq_ref[...] = jnp.sum(sq_in[...], axis=0)


def local(n, queries, keys, values, out_weight, latent, valid, timestep):
    rows, features = queries.shape
    channels = out_weight.shape[0]
    heads = features // HEAD_DIM
    mine = heads // UNIT
    held = UNIT + 2 * R_WIN
    hbm = pl.BlockSpec(memory_space=pl.ANY)
    vmem = pl.BlockSpec(memory_space=pltpu.VMEM)
    dma = pltpu.SemaphoreType.DMA
    vel, squares = pl.pallas_call(
        functools.partial(kernel, n),
        out_shape=(jax.ShapeDtypeStruct((channels, rows), F32),
                   jax.ShapeDtypeStruct((8, rows), F32)),
        in_specs=[hbm, hbm, hbm, vmem, pl.BlockSpec(memory_space=pltpu.SMEM)],
        out_specs=(vmem, vmem),
        scratch_shapes=[
            pltpu.VMEM((rows, features), BF16),
            pltpu.VMEM((heads, channels, rows), BF16),
            pltpu.VMEM((mine, UNIT, rows, HEAD_DIM), BF16),
            pltpu.VMEM((mine, held, rows, HEAD_DIM), BF16),
            pltpu.VMEM((mine, held, channels, rows), BF16),
            pltpu.VMEM((2, 2 * R_WIN + 1, rows, rows), F32),
            pltpu.VMEM((UNIT, channels, rows), F32),
            pltpu.VMEM((UNIT - 1, channels, rows), F32),
            pltpu.VMEM((n, 8, rows), F32),
            dma((3, mine)),
            dma,
            dma((UNIT - 1, 3, mine)),
            dma((UNIT - 1, 3, mine)),
            dma((2, 2, mine)),
            dma((2, 2, mine)),
            dma((UNIT - 1,)),
            dma((UNIT - 1,)),
            dma((n,)),
            dma((n,)),
        ],
        compiler_params=pltpu.CompilerParams(
            collective_id=0, has_side_effects=True, vmem_limit_bytes=40 * 1024 * 1024),
    )(queries, keys, values, out_weight, valid)
    count = jnp.float32(channels) * jnp.sum(valid.astype(jnp.float32))
    rms = jnp.sqrt(jnp.sum(squares) / count + 1e-06)
    velocity = vel / rms
    level = timestep[0].astype(jnp.float32)
    early = 1.0 - level / STEPS
    later = 1.0 - (level + 1.0) / STEPS
    sigma_early = 5.0 * early / (1.0 + 4.0 * early)
    sigma_later = 5.0 * later / (1.0 + 4.0 * later)
    return (velocity, latent + (sigma_later - sigma_early) * velocity)


def solution(mesh):
    tokens = P(("groups", "blk"), None)
    spread = P(None, ("groups", "blk"))
    return jax.shard_map(
        functools.partial(local, mesh.shape["blk"]), mesh=mesh,
        in_specs=(tokens, tokens, tokens, P(), spread, P("groups"), P("groups")),
        out_specs=(spread, spread), check_vma=False)
```

time: 175 us -> 68.3 us (0.39)
  starting transfers between devices: 64.8 us -> 0 us
  Pallas kernels: 0 us -> 57.1 us
  blocking collectives: 43.2 us -> 0 us
  matrix products: 36.4 us -> 0 us
  local copies, waits for them, and re-layouts: 14.6 us -> 5.57 us
  other arithmetic: 9.02 us -> 2.53 us
  between operations: 6.28 us -> 2.75 us
    ppermute x8 -> x0, starting transfers between devices: 64.8 us -> none  [shifted(): return lax.ppermute(shard, axis, pairs)]
    pallas_call x0 -> x1, Pallas kernels: none -> 57.1 us  [local(): pl.pallas_call(functools.partial(kernel, n), out_shape=(jax.ShapeDtypeStr...]
    psum x1 -> x0, blocking collectives: 43.2 us -> none  [local(): squares = lax.psum(jnp.sum(vel * vel), 'blk')]
    dot_general x11 -> x0, matrix products: 36.4 us -> none  [the longest x5 21.4 us: weighted(): jnp.einsum('hqk,khd->hqd', weights.astype(jnp.bfloat16), value_heads, pre...]
    ppermute x4 -> x0, local copies, waits for them, and re-layouts: 8.15 us -> none  [shifted(): return lax.ppermute(shard, axis, pairs)]
    reduce_sum x4 -> x2, other arithmetic: 7.3 us -> 1.86 us  [the longest x1 1.26 us: local(): count = jnp.float32(channels) * jnp.sum(valid.astype(jnp.float32))]
    unnamed x25 -> x12, local copies, waits for them, and re-layouts: 5.73 us -> 5.57 us
  transfers between devices with their start and end apart: 8 -> 0, of which waited for: 0 -> 0; matrix products, arithmetic and copies ran while one was open for 27% -> 0% of each run, Pallas kernels for 0% -> 0%
where the time goes in v1:
time: 68.3 us; the launch traced here: 68 us
  Pallas kernels  57.1 us (84%)
  local copies, waits for them, and re-layouts  5.57 us (8%)
  between operations  2.75 us (4%)
  other arithmetic  2.53 us (4%)
    pallas_call x1, Pallas kernels, local(): pl.pallas_call(functools.partial(kernel, n), out_shape=(jax.ShapeDtypeStr...  57.1 us
    unnamed x12, local copies, waits for them, and re-layouts  5.57 us

profile of v1, /device:TPU:0, one launch (start us, length us, event | category | flops | bytes accessed | tf_op | source)
XLA Modules:
  0.0 68.0 jit_solution(13279337090131307562)
XLA Ops:
  1.4 1.3 %convert_reduce_fusion = f32[]{:T(128)} fusion(s32[16]{0:T(128)} %valid_ref.1), kind=kLoop, calls=%fused_computation.2 | loop fusion | flops 31 | bytes 68 | tf_op jit(solution)/shard_map/reduce_sum | solution.py:277
  3.3 0.0 copy-start
  3.3 1.3 %copy-done = bf16[256,2560]{1,0:T(8,128)(2,1)S(1)} copy-done((bf16[256,2560]{1,0:T(8,128)(2,1)S(1)}, bf16[256,2560]{1,0:T(8,128)(2,1)}, u32[]{:S(2)}) %copy-start) | copy-done | bytes 1310744
  4.6 0.0 copy-start.1
  4.6 1.3 %copy-done.1 = bf16[256,2560]{1,0:T(8,128)(2,1)S(1)} copy-done((bf16[256,2560]{1,0:T(8,128)(2,1)S(1)}, bf16[256,2560]{1,0:T(8,128)(2,1)}, u32[]{:S(2)}) %copy-start.1) | copy-done | bytes 1310744
  5.9 0.0 copy-start.2
  5.9 1.3 %copy-done.2 = bf16[256,2560]{1,0:T(8,128)(2,1)S(1)} copy-done((bf16[256,2560]{1,0:T(8,128)(2,1)S(1)}, bf16[256,2560]{1,0:T(8,128)(2,1)}, u32[]{:S(2)}) %copy-start.2) | copy-done | bytes 1310744
  7.2 0.0 copy-start.3
  7.2 1.0 %copy-done.3 = bf16[64,2560]{1,0:T(8,128)(2,1)S(1)} copy-done((bf16[64,2560]{1,0:T(8,128)(2,1)S(1)}, bf16[64,2560]{1,0:T(8,128)(2,1)}, u32[]{:S(2)}) %copy-start.3) | copy-done | bytes 327704
  8.2 0.0 copy-start.4
  8.2 0.7 copy-done.4
  8.9 0.0 copy-start.5
  8.9 57.1 %shard_map.86 = (f32[64,256]{1,0:T(8,128)S(1)}, f32[8,256]{1,0:T(8,128)S(1)}) custom-call(bf16[256,2560]{1,0:T(8,128)(2,1)S(1)} %copy-done, bf16[256,2560]{1,0:T(8,128)(2,1)S(1)} %copy-done.1, bf16[256,2560]{1,0:T(8,128)(2,1)S(1)} %copy-done.2, bf16[64,2560]{1,0:T(8,128)(2,1)S(1)} %copy-done.3, s32[16]{0:T(128)S(1)} %copy-done.4), custom_call_target="tpu_custom_call" | custom-call | tf_op jit(solution)/shard_map/pallas_call | solution.py:247
  66.0 0.6 reduce_sum.18
  67.3 0.0 copy-done.5
  67.3 0.7 multiply_add_fusion
Async XLA Ops:
  3.3 1.3 %copy-start = (bf16[256,2560]{1,0:T(8,128)(2,1)S(1)}, bf16[256,2560]{1,0:T(8,128)(2,1)}, u32[]{:S(2)}) copy-start(bf16[256,2560]{1,0:T(8,128)(2,1)} %q_hbm.1) | copy-start | bytes 3932164
  4.6 1.3 %copy-start.1 = (bf16[256,2560]{1,0:T(8,128)(2,1)S(1)}, bf16[256,2560]{1,0:T(8,128)(2,1)}, u32[]{:S(2)}) copy-start(bf16[256,2560]{1,0:T(8,128)(2,1)} %k_hbm.1) | copy-start | bytes 3932164
  5.9 1.3 %copy-start.2 = (bf16[256,2560]{1,0:T(8,128)(2,1)S(1)}, bf16[256,2560]{1,0:T(8,128)(2,1)}, u32[]{:S(2)}) copy-start(bf16[256,2560]{1,0:T(8,128)(2,1)} %v_hbm.1) | copy-start | bytes 3932164
  7.2 1.0 %copy-start.3 = (bf16[64,2560]{1,0:T(8,128)(2,1)S(1)}, bf16[64,2560]{1,0:T(8,128)(2,1)}, u32[]{:S(2)}) copy-start(bf16[64,2560]{1,0:T(8,128)(2,1)} %w_ref.1) | copy-start | bytes 983044
  8.2 0.7 copy-start.4
  8.9 58.4 %copy-start.5 = (f32[64,256]{1,0:T(8,128)S(1)}, f32[64,256]{1,0:T(8,128)}, u32[]{:S(2)}) copy-start(f32[64,256]{1,0:T(8,128)} %param.11) | copy-start | bytes 196612

commit v2 on v1

--- a/solution.py
+++ b/solution.py
@@ -16,9 +16,9 @@
 LOG2E = 1.4426950408889634
 
 
-def kernel(n, q_hbm, k_hbm, v_hbm, w_ref, valid_ref, vel_ref, sq_ref,
-           v_buf, vw_own, qbuf, kbuf, vwbuf, s_buf, vel_acc, vel_in, sq_in,
-           loc_sem, v_sem, xs_sem, xr_sem, zs_sem, zr_sem, vs_sem, vr_sem, ss_sem, sr_sem):
+def kernel(n, q_hbm, k_hbm, v_hbm, w_hbm, valid_ref, step_ref, vel_ref, scale_ref, dt_ref,
+           v_buf, w_buf, vw_own, qbuf, kbuf, vwbuf, s_buf, vel_acc, vel_out, vel_in, sq_in,
+           loc_sem, v_sem, w_sem, xs_sem, xr_sem, zs_sem, zr_sem, vs_sem, vr_sem, ss_sem, sr_sem):
     rows = q_hbm.shape[0]
     heads = q_hbm.shape[1] // HEAD_DIM
     mine = heads // UNIT
@@ -31,12 +31,30 @@
 
     barrier = pltpu.get_barrier_semaphore()
 
-    @pl.loop(1, n)
-    def _(d):
-        pl.semaphore_signal(barrier, inc=1, device_id={"blk": (me + d) % n},
+    def greet(device):
+        pl.semaphore_signal(barrier, inc=1, device_id={"blk": device},
                             device_id_type=pl.DeviceIdType.MESH)
 
+    near = units - 1 <= mine
+    if near:
+        for d in (1, 2, 3):
+            greet(unit * UNIT + partner[d])
+
+        @pl.when(unit < units - 1)
+        def _():
+            greet(me + UNIT)
+
+        @pl.when(unit > 0)
+        def _():
+            greet(me - UNIT)
+    else:
+        @pl.loop(1, n)
+        def _(d):
+            greet((me + d) % n)
+
     v_copy = pltpu.make_async_copy(v_hbm, v_buf, v_sem)
+    w_copy = pltpu.make_async_copy(w_hbm, w_buf, w_sem)
+    w_copy.start()
     v_copy.start()
 
     def columns(t, j):
@@ -90,27 +108,31 @@
         vwbuf[:, R_WIN + UNIT:] = jnp.zeros((mine, R_WIN) + vwbuf.shape[2:], BF16)
 
     vel_acc[...] = jnp.zeros_like(vel_acc)
+    if near:
+        pl.semaphore_wait(barrier, UNIT - 1 + (unit + units - 1) // units
+                          + (2 * units - 2 - unit) // units)
+    else:
+        pl.semaphore_wait(barrier, n - 1)
+
+    def send_all(kind):
+        @pl.loop(0, mine)
+        def _(j):
+            for d in (2, 3, 1):
+                cross(d, j, kind).start()
+
+    send_all(0)
+    w_copy.wait()
     v_copy.wait()
     for h in range(heads):
         cols = slice(h * HEAD_DIM, (h + 1) * HEAD_DIM)
         vw_own[h] = lax.dot_general(
-            w_ref[:, cols], v_buf[:, cols], NT, preferred_element_type=F32).astype(BF16)
-
-    pl.semaphore_wait(barrier, n - 1)
-
-    @pl.loop(0, mine + 1)
+            w_buf[:, cols], v_buf[:, cols], NT, preferred_element_type=F32).astype(BF16)
+    send_all(1)
+    send_all(2)
+
+    @pl.loop(0, mine)
     def _(j):
-        @pl.when(j < mine)
-        def _():
-            for kind in (0, 1):
-                for d in (2, 3, 1):
-                    cross(d, j, kind).start()
-            local(j, 1).start()
-
-        @pl.when(j > 0)
-        def _():
-            for d in (2, 3, 1):
-                cross(d, j - 1, 2).start()
+        local(j, 1).start()
 
     limits = []
     for kb in range(UNIT + 2 * R_WIN):
@@ -120,9 +142,9 @@
     factor = LOG2E / (HEAD_DIM ** 0.5)
     masked = (0, 1, R_WIN + UNIT - 1, R_WIN + UNIT, R_WIN + UNIT + 1)
 
-    def attend(j):
+    def attend(j, blocks, after=None):
         row_id = lax.broadcasted_iota(jnp.int32, (rows, rows), 0)
-        for qs in range(UNIT):
+        for qs in blocks:
             queries = qbuf[j, qs]
             top = None
             for kk in range(2 * R_WIN + 1):
@@ -142,58 +164,88 @@
                 o = jnp.dot(vwbuf[j, qs + kk], e.astype(BF16), preferred_element_type=F32)
                 out = o if out is None else out + o
             vel_acc[qs] += out / total
-
-    @pl.loop(0, mine + 1)
-    def _(j):
-        @pl.when(j < mine)
-        def _():
-            for kind in (0, 1):
-                local(j, kind).wait()
-                for d in (1, 2, 3):
-                    cross(d, j, kind).wait_recv()
+            if after is not None:
+                after(j, qs)
+
+    def arrive(j, kind):
+        @pl.when(unit > 0)
+        def _():
+            along(True, j, kind).wait_recv()
+
+        @pl.when(unit < units - 1)
+        def _():
+            along(False, j, kind).wait_recv()
+
+    for kind in (0, 1):
+        @pl.loop(0, mine)
+        def _(j):
+            if kind == 1:
+                @pl.when(j < 2)
+                def _():
+                    arrive(mine - 2 + j, 0)
+
+            @pl.when(j >= 2)
+            def _():
+                arrive(j - 2, kind)
+
+            local(j, kind).wait()
+            for d in (1, 2, 3):
+                cross(d, j, kind).wait_recv()
 
             @pl.when(unit < units - 1)
             def _():
-                along(True, j, 0).start()
-                along(True, j, 1).start()
+                along(True, j, kind).start()
 
             @pl.when(unit > 0)
             def _():
-                along(False, j, 0).start()
-                along(False, j, 1).start()
-
-        @pl.when(j > 0)
-        def _():
-            i = j - 1
-            local(i, 2).wait()
-            for d in (1, 2, 3):
-                cross(d, i, 2).wait_recv()
-
-            @pl.when(unit > 0)
-            def _():
-                along(True, i, 0).wait_recv()
-                along(True, i, 1).wait_recv()
-
-            @pl.when(unit < units - 1)
-            def _():
-                along(False, i, 0).wait_recv()
-                along(False, i, 1).wait_recv()
-
-            attend(i)
-
-    def give(d):
+                along(False, j, kind).start()
+
+    def give(qs, d):
         return pltpu.make_async_remote_copy(
-            src_ref=vel_acc.at[partner[d]], dst_ref=vel_in.at[d - 1],
+            src_ref=vel_out.at[qs], dst_ref=vel_in.at[d - 1],
             send_sem=vs_sem.at[d - 1], recv_sem=vr_sem.at[d - 1],
-            device_id={"blk": unit * UNIT + partner[d]},
+            device_id={"blk": unit * UNIT + qs},
             device_id_type=pl.DeviceIdType.MESH)
 
-    for d in (2, 3, 1):
-        give(d).start()
+    def hand_over(j, qs):
+        @pl.when(j == mine - 1)
+        def _():
+            vel_out[qs] = vel_acc[qs].astype(BF16)
+            give(qs, 2 + (qs + core) % 2).start()
+
+    for j in (mine - 2, mine - 1):
+        arrive(j, 1)
+
+    def own_chip(blocks):
+        @pl.loop(0, mine)
+        def _(j):
+            local(j, 2).wait()
+            cross(1, j, 2).wait_recv()
+            attend(j, blocks)
+
+    def other_chip(blocks):
+        @pl.loop(0, mine)
+        def _(j):
+            for d in (2, 3):
+                cross(d, j, 2).wait_recv()
+            attend(j, blocks, hand_over)
+
+    @pl.when(chip == 0)
+    def _():
+        own_chip((0, 1))
+        other_chip((2, 3))
+
+    @pl.when(chip == 1)
+    def _():
+        own_chip((2, 3))
+        other_chip((0, 1))
+
+    vel_out[partner[1]] = vel_acc[partner[1]].astype(BF16)
+    give(partner[1], 1).start()
     vel = vel_acc[slot]
     for d in (1, 2, 3):
-        give(d).wait_recv()
-        vel = vel + vel_in[d - 1]
+        give(partner[d], d).wait_recv()
+        vel = vel + vel_in[d - 1].astype(F32)
     col_id = lax.broadcasted_iota(jnp.int32, vel.shape, 1)
     vel = jnp.where(col_id < valid_ref[me], vel, F32(0))
     vel_ref[...] = vel
@@ -226,13 +278,23 @@
             along(False, j, 1).wait_send()
 
     for d in (1, 2, 3):
-        give(d).wait_send()
+        give(partner[d], d).wait_send()
 
     @pl.loop(1, n)
     def _(d):
         tell(d).wait()
 
-    sq_ref[...] = jnp.sum(sq_in[...], axis=0)
+    squares = jnp.sum(jnp.sum(sq_in[...], axis=0), keepdims=True)
+    used = lax.fori_loop(0, n, lambda b, acc: acc + valid_ref[b], jnp.int32(0))
+    wide = vel.shape
+    count = jnp.full(wide, used, jnp.int32).astype(F32) * vel.shape[0]
+    scale_ref[...] = 1.0 / jnp.sqrt(jnp.broadcast_to(squares, wide) / count + 1e-06)
+    level = jnp.full(wide, step_ref[0], jnp.int32).astype(F32)
+    early = 1.0 - level / STEPS
+    later = 1.0 - (level + 1.0) / STEPS
+    sigma_early = 5.0 * early / (1.0 + 4.0 * early)
+    sigma_later = 5.0 * later / (1.0 + 4.0 * later)
+    dt_ref[...] = sigma_later - sigma_early
 
 
 def local(n, queries, keys, values, out_weight, latent, valid, timestep):
@@ -243,24 +305,27 @@
     held = UNIT + 2 * R_WIN
     hbm = pl.BlockSpec(memory_space=pl.ANY)
     vmem = pl.BlockSpec(memory_space=pltpu.VMEM)
+    smem = pl.BlockSpec(memory_space=pltpu.SMEM)
     dma = pltpu.SemaphoreType.DMA
-    vel, squares = pl.pallas_call(
+    vel, scale, dt = pl.pallas_call(
         functools.partial(kernel, n),
-        out_shape=(jax.ShapeDtypeStruct((channels, rows), F32),
-                   jax.ShapeDtypeStruct((8, rows), F32)),
-        in_specs=[hbm, hbm, hbm, vmem, pl.BlockSpec(memory_space=pltpu.SMEM)],
-        out_specs=(vmem, vmem),
+        out_shape=(jax.ShapeDtypeStruct((channels, rows), F32),) * 3,
+        in_specs=[hbm, hbm, hbm, hbm, smem, smem],
+        out_specs=(vmem,) * 3,
         scratch_shapes=[
             pltpu.VMEM((rows, features), BF16),
+            pltpu.VMEM((channels, features), BF16),
             pltpu.VMEM((heads, channels, rows), BF16),
             pltpu.VMEM((mine, UNIT, rows, HEAD_DIM), BF16),
             pltpu.VMEM((mine, held, rows, HEAD_DIM), BF16),
             pltpu.VMEM((mine, held, channels, rows), BF16),
             pltpu.VMEM((2, 2 * R_WIN + 1, rows, rows), F32),
             pltpu.VMEM((UNIT, channels, rows), F32),
-            pltpu.VMEM((UNIT - 1, channels, rows), F32),
+            pltpu.VMEM((UNIT, channels, rows), BF16),
+            pltpu.VMEM((UNIT - 1, channels, rows), BF16),
             pltpu.VMEM((n, 8, rows), F32),
             dma((3, mine)),
+            dma,
             dma,
             dma((UNIT - 1, 3, mine)),
             dma((UNIT - 1, 3, mine)),
@@ -272,17 +337,10 @@
             dma((n,)),
         ],
         compiler_params=pltpu.CompilerParams(
-            collective_id=0, has_side_effects=True, vmem_limit_bytes=40 * 1024 * 1024),
-    )(queries, keys, values, out_weight, valid)
-    count = jnp.float32(channels) * jnp.sum(valid.astype(jnp.float32))
-    rms = jnp.sqrt(jnp.sum(squares) / count + 1e-06)
-    velocity = vel / rms
-    level = timestep[0].astype(jnp.float32)
-    early = 1.0 - level / STEPS
-    later = 1.0 - (level + 1.0) / STEPS
-    sigma_early = 5.0 * early / (1.0 + 4.0 * early)
-    sigma_later = 5.0 * later / (1.0 + 4.0 * later)
-    return (velocity, latent + (sigma_later - sigma_early) * velocity)
+            collective_id=0, has_side_effects=True, vmem_limit_bytes=67043328),
+    )(queries, keys, values, out_weight, valid, timestep)
+    velocity = vel * scale
+    return (velocity, latent + dt * velocity)
 
 
 def solution(mesh):

time: 68.3 us -> 60.3 us (0.88)
  local copies, waits for them, and re-layouts: 5.57 us -> 0 us
  between operations: 2.75 us -> 1.29 us
  other arithmetic: 2.53 us -> 1.6 us
    unnamed x12 -> x0, local copies, waits for them, and re-layouts: 5.57 us -> none
    reduce_sum x2 -> x0, other arithmetic: 1.86 us -> none  [the longest x1 1.26 us: local(): count = jnp.float32(channels) * jnp.sum(valid.astype(jnp.float32))]
    add x1, other arithmetic: 0.67 us -> 1.6 us  [local(): return (velocity, latent + dt * velocity)]
where the time goes in v2:
time: 60.3 us; the launch traced here: 60.1 us
  Pallas kernels  57.3 us (95%)
  other arithmetic  1.6 us (3%)
  between operations  1.29 us (2%)
    pallas_call x1, Pallas kernels, local(): pl.pallas_call(functools.partial(kernel, n), out_shape=(jax.ShapeDtypeStr...  57.3 us
    add x1, other arithmetic, local(): return (velocity, latent + dt * velocity)  1.6 us

profile of v2, /device:TPU:0, one launch (start us, length us, event | category | flops | bytes accessed | tf_op | source)
XLA Modules:
  0.0 60.1 jit_solution(11042136285593404176)
XLA Ops:
  1.3 57.3 %shard_map.86 = (f32[64,256]{1,0:T(8,128)}, f32[64,256]{1,0:T(8,128)}, f32[64,256]{1,0:T(8,128)}) custom-call(bf16[256,2560]{1,0:T(8,128)(2,1)} %q_hbm.1, bf16[256,2560]{1,0:T(8,128)(2,1)} %k_hbm.1, bf16[256,2560]{1,0:T(8,128)(2,1)} %v_hbm.1, bf16[64,2560]{1,0:T(8,128)(2,1)} %w_hbm.1, s32[16]{0:T(128)} %valid_ref.1, s32[1]{0:T(128)S(6)} %copy.9.step_ref), custom_call_target="tpu_custom_call" | custom-call | tf_op jit(solution)/shard_map/pallas_call | solution.py:310
  58.5 1.6 %multiply_add_fusion = (f32[64,256]{1,0:T(8,128)}, f32[64,256]{1,0:T(8,128)}) fusion(f32[64,256]{1,0:T(8,128)} %param.11, f32[64,256]{1,0:T(8,128)} %get-tuple-element.7, f32[64,256]{1,0:T(8,128)} %get-tuple-element.5, f32[64,256]{1,0:T(8,128)} %get-tuple-element.6), kind=kLoop, calls=%fused_computation | loop fusion | flops 49152 | bytes 393216 | tf_op jit(solution)/shard_map/add | solution.py:343

commit v3 on v2

--- a/solution.py
+++ b/solution.py
@@ -35,7 +35,7 @@
         pl.semaphore_signal(barrier, inc=1, device_id={"blk": device},
                             device_id_type=pl.DeviceIdType.MESH)
 
-    near = units - 1 <= mine
+    near = 2 * (units - 1) <= mine + 1
     if near:
         for d in (1, 2, 3):
             greet(unit * UNIT + partner[d])
@@ -114,25 +114,38 @@
     else:
         pl.semaphore_wait(barrier, n - 1)
 
-    def send_all(kind):
-        @pl.loop(0, mine)
-        def _(j):
-            for d in (2, 3, 1):
-                cross(d, j, kind).start()
-
-    send_all(0)
+    def send(j, kind):
+        for d in (2, 3, 1):
+            cross(d, j, kind).start()
+
+    early = min(2, mine)
+    for j in range(early):
+        send(j, 0)
+
+    @pl.loop(0, mine)
+    def _(j):
+        cross(1, j, 2).start()
+
     w_copy.wait()
     v_copy.wait()
     for h in range(heads):
         cols = slice(h * HEAD_DIM, (h + 1) * HEAD_DIM)
         vw_own[h] = lax.dot_general(
             w_buf[:, cols], v_buf[:, cols], NT, preferred_element_type=F32).astype(BF16)
-    send_all(1)
-    send_all(2)
 
     @pl.loop(0, mine)
     def _(j):
         local(j, 1).start()
+        send(j, 1)
+
+        @pl.when(j + early < mine)
+        def _():
+            send(j + early, 0)
+
+    @pl.loop(0, mine)
+    def _(j):
+        for d in (2, 3):
+            cross(d, j, 2).start()
 
     limits = []
     for kb in range(UNIT + 2 * R_WIN):
@@ -176,18 +189,8 @@
         def _():
             along(False, j, kind).wait_recv()
 
-    for kind in (0, 1):
-        @pl.loop(0, mine)
-        def _(j):
-            if kind == 1:
-                @pl.when(j < 2)
-                def _():
-                    arrive(mine - 2 + j, 0)
-
-            @pl.when(j >= 2)
-            def _():
-                arrive(j - 2, kind)
-
+    def gather(j):
+        for kind in (0, 1):
             local(j, kind).wait()
             for d in (1, 2, 3):
                 cross(d, j, kind).wait_recv()
@@ -213,15 +216,21 @@
             vel_out[qs] = vel_acc[qs].astype(BF16)
             give(qs, 2 + (qs + core) % 2).start()
 
-    for j in (mine - 2, mine - 1):
-        arrive(j, 1)
-
     def own_chip(blocks):
-        @pl.loop(0, mine)
+        @pl.loop(0, mine + 1)
         def _(j):
-            local(j, 2).wait()
-            cross(1, j, 2).wait_recv()
-            attend(j, blocks)
+            @pl.when(j < mine)
+            def _():
+                gather(j)
+
+            @pl.when(j > 0)
+            def _():
+                i = j - 1
+                arrive(i, 0)
+                arrive(i, 1)
+                local(i, 2).wait()
+                cross(1, i, 2).wait_recv()
+                attend(i, blocks)
 
     def other_chip(blocks):
         @pl.loop(0, mine)
@@ -230,18 +239,22 @@
                 cross(d, j, 2).wait_recv()
             attend(j, blocks, hand_over)
 
+    def on_chip():
+        vel_out[partner[1]] = vel_acc[partner[1]].astype(BF16)
+        give(partner[1], 1).start()
+
     @pl.when(chip == 0)
     def _():
         own_chip((0, 1))
+        on_chip()
         other_chip((2, 3))
 
     @pl.when(chip == 1)
     def _():
         own_chip((2, 3))
+        on_chip()
         other_chip((0, 1))
 
-    vel_out[partner[1]] = vel_acc[partner[1]].astype(BF16)
-    give(partner[1], 1).start()
     vel = vel_acc[slot]
     for d in (1, 2, 3):
         give(partner[d], d).wait_recv()
@@ -249,7 +262,9 @@
     col_id = lax.broadcasted_iota(jnp.int32, vel.shape, 1)
     vel = jnp.where(col_id < valid_ref[me], vel, F32(0))
     vel_ref[...] = vel
-    sq_in[0] = jnp.sum((vel * vel).reshape(vel.shape[0] // 8, 8, vel.shape[1]), axis=0)
+    square = jnp.sum(vel * vel, axis=0, keepdims=True)
+    lanes = sq_in.shape[2]
+    sq_in[0] = sum(square[:, i:i + lanes] for i in range(0, square.shape[1], lanes))
 
     def tell(d):
         return pltpu.make_async_remote_copy(
@@ -323,7 +338,7 @@
             pltpu.VMEM((UNIT, channels, rows), F32),
             pltpu.VMEM((UNIT, channels, rows), BF16),
             pltpu.VMEM((UNIT - 1, channels, rows), BF16),
-            pltpu.VMEM((n, 8, rows), F32),
+            pltpu.VMEM((n, 1, HEAD_DIM), F32),
             dma((3, mine)),
             dma,
             dma,

time: 60.3 us -> 55.6 us (0.922)
  Pallas kernels: 57.3 us -> 52.5 us
    pallas_call x1, Pallas kernels: 57.3 us -> 52.5 us  [local(): pl.pallas_call(functools.partial(kernel, n), out_shape=(jax.ShapeDtypeStr...]
where the time goes in v3:
time: 55.6 us; the launch traced here: 55.4 us
  Pallas kernels  52.5 us (94%)
  other arithmetic  1.6 us (3%)
  between operations  1.29 us (2%)
    pallas_call x1, Pallas kernels, local(): pl.pallas_call(functools.partial(kernel, n), out_shape=(jax.ShapeDtypeStr...  52.5 us
    add x1, other arithmetic, local(): return (velocity, latent + dt * velocity)  1.6 us

profile of v3, /device:TPU:0, one launch (start us, length us, event | category | flops | bytes accessed | tf_op | source)
XLA Modules:
  0.0 55.4 jit_solution(2053404625661820098)
XLA Ops:
  1.3 52.5 %shard_map.86 = (f32[64,256]{1,0:T(8,128)}, f32[64,256]{1,0:T(8,128)}, f32[64,256]{1,0:T(8,128)}) custom-call(bf16[256,2560]{1,0:T(8,128)(2,1)} %q_hbm.1, bf16[256,2560]{1,0:T(8,128)(2,1)} %k_hbm.1, bf16[256,2560]{1,0:T(8,128)(2,1)} %v_hbm.1, bf16[64,2560]{1,0:T(8,128)(2,1)} %w_hbm.1, s32[16]{0:T(128)} %valid_ref.1, s32[1]{0:T(128)S(6)} %copy.9.step_ref), custom_call_target="tpu_custom_call" | custom-call | tf_op jit(solution)/shard_map/pallas_call | solution.py:325
  53.8 1.6 %multiply_add_fusion = (f32[64,256]{1,0:T(8,128)}, f32[64,256]{1,0:T(8,128)}) fusion(f32[64,256]{1,0:T(8,128)} %param.11, f32[64,256]{1,0:T(8,128)} %get-tuple-element.7, f32[64,256]{1,0:T(8,128)} %get-tuple-element.5, f32[64,256]{1,0:T(8,128)} %get-tuple-element.6), kind=kLoop, calls=%fused_computation | loop fusion | flops 49152 | bytes 393216 | tf_op jit(solution)/shard_map/add | solution.py:358
